TPU v7x, 32 devices: a whole 2x2x4 slice. The times are simulated.
32 devices in a mesh: pipe: 4 (over z), dp: 2 (over core), expert: 4 (over y, x).
Axes of the slice: x: 2, y: 2, z: 4, core: 2. Of those that a mesh axis runs over, the one named last changes fastest.
Arguments:
- cotangent: bfloat16 [4, 512, 7168], P('pipe', ('dp', 'expert')), may hold values from -6 to 6
- routes: int32 [4, 2, 512, 8], P('pipe', None, ('dp', 'expert')), may hold values from 0 to 255, as said below
- gates: bfloat16 [4, 2, 512, 8], P('pipe', None, ('dp', 'expert')), may hold values from 0.099609375 to 1
- gate_pre: bfloat16 [4, 2, 2, 4, 2, 4096], P('pipe', None, 'dp', None, None, 'expert'), may hold values from -6 to 6
- up_pre: bfloat16 [4, 2, 2, 4, 2, 4096], P('pipe', None, 'dp', None, None, 'expert'), may hold values from -6 to 6
- w_gate: bfloat16 [4, 7168, 4096], P('pipe', None, 'expert'), may hold values from -0.0625 to 0.0625
- w_up: bfloat16 [4, 7168, 4096], P('pipe', None, 'expert'), may hold values from -0.0625 to 0.0625
- w_down: bfloat16 [4, 4096, 7168], P('pipe', 'expert'), may hold values from -0.125 to 0.125
Outputs:
- down_grad: float32 [4, 4096, 7168], P('pipe', 'expert', 'dp')
Inputs may be any that keep to these rules, and one draw needn't show every extreme that they name: `routes`: each token names 8 different experts. At one section and step the tokens of one device name each of the experts 0 to 1 at least once and at most 2 times; at every section and step, in some replica every device names one of them exactly 2 times.
All inputs are finite; a program needn't handle non-finite values.
Results may differ from a plain program's by a relative error of at most 0.0095.
Values may be sent and summed in bfloat16 or wider, within the bound.
A program may use at most 128 MiB of HBM per device.

v0:
```python
import functools

import jax
import jax.numpy as jnp
from jax import lax
from jax.experimental import pallas as pl
from jax.experimental.pallas import tpu as pltpu
from jax.sharding import PartitionSpec as P

EXP_FL = 2
STEPS = 2
LANES = 128
MESH = pl.DeviceIdType.MESH
F32 = jnp.float32
BF16 = jnp.bfloat16


def contract_last(left, right):
    return lax.dot_general(
        left, right, (((1,), (1,)), ((), ())), preferred_element_type=F32
    )


def steps_of(size):
    for count in range(2, size // 32 + 1, 2):
        if size % count == 0 and size // count % 16 == 0 and size // count <= 448:
            return size // count
    return 0


def rows_dot(x, weight, start, size, columns):
    m = x.shape[0]
    held = (size // 2 - m // 2) // 16 * 16
    right = jnp.concatenate([weight[start : start + held, columns], x], axis=0)
    left = jnp.concatenate([x, weight[start + held : start + size, columns]], axis=0)
    return contract_last(left, right)


def rows_out(both, m):
    held = both.shape[1] - m
    low = held // LANES * LANES
    streamed = both[m:, low : held + m].T[held - low :, :]
    return jnp.concatenate([both[0:m, 0:held], streamed], axis=1)


def slot_table(ids, weights, capacity):
    topk, tokens = ids.shape
    row = lax.broadcasted_iota(jnp.int32, (8, tokens), 0)
    expert = row // capacity
    hit = jnp.zeros((8, tokens), F32)
    gate = jnp.zeros((8, tokens), F32)
    for k in range(topk):
        match = ids[k : k + 1, :] == expert
        hit = jnp.where(match, 1.0, hit)
        gate = gate + jnp.where(match, weights[k : k + 1, :], 0.0)
    upto = (
        lax.broadcasted_iota(jnp.int32, (tokens, tokens), 0)
        <= lax.broadcasted_iota(jnp.int32, (tokens, tokens), 1)
    ).astype(F32)
    rank = jnp.dot(hit.astype(BF16), upto.astype(BF16), preferred_element_type=F32) - 1.0
    valid = (rank == (row % capacity).astype(F32)) & (row < EXP_FL * capacity)
    select = jnp.where(valid, hit, 0.0)
    slot_gate = jnp.sum(select * gate, axis=1, keepdims=True)
    return select, jnp.broadcast_to(slot_gate, (8, LANES))


def kernel(
    dims,
    cot_hbm,
    routes_hbm,
    gates_hbm,
    pre_u,
    pre_v,
    w_gate,
    w_up,
    w_down,
    out_rows,
    out_scaled,
    cot,
    routes,
    gates,
    wd,
    wg,
    wu,
    got_u,
    got_v,
    stage_u,
    stage_v,
    send_rows,
    recv_rows,
    stage_x,
    sel_send,
    sel_recv,
    base_send,
    base_recv,
    acc_send,
    acc_recv,
    part_send,
    part_recv,
    fin_stage,
    fin_send,
    fin_recv,
    cot_sem,
    w_sem,
    pre_ss,
    pre_rs,
    rows_ss,
    rows_rs,
    sel_ss,
    sel_rs,
    base_ss,
    base_rs,
    acc_ss,
    acc_rs,
    part_ss,
    part_rs,
    fin_ss,
    fin_rs,
):
    n_pipe, n_dp, n_exp, cap, width, hidden, n_ch = dims
    half = width // n_dp
    ch = half // n_ch
    split = n_exp // EXP_FL
    n_src = n_dp * n_exp
    slots = n_src * cap
    group = n_dp * cap
    n_h, part_h = acc_send.shape[0], acc_send.shape[2]
    step_h, step_c = steps_of(part_h), steps_of(ch)
    fast = slots == 16 and step_h > 64 and step_c > 64 and part_h % LANES == 0
    p, r, j = lax.axis_index("pipe"), lax.axis_index("dp"), lax.axis_index("expert")
    me = j * n_dp + r

    def at(pipe, dp, expert):
        return {"pipe": pipe, "dp": dp, "expert": expert}

    def remote(src, dst, ss, rs, where):
        return pltpu.make_async_remote_copy(
            src_ref=src, dst_ref=dst, send_sem=ss, recv_sem=rs, device_id=where, device_id_type=MESH
        )

    def weight_copies():
        downs, outs = [], []
        for k in range(n_ch):
            at_col = pl.multiple_of(r * half + k * ch, LANES)
            downs.append(
                pltpu.make_async_copy(w_down.at[0, :, pl.ds(at_col, ch)], wd.at[k], w_sem.at[0, k])
            )
        for k in range(n_ch):
            at_col = pl.multiple_of(r * half + k * ch, LANES)
            outs.append(
                (
                    pltpu.make_async_copy(w_gate.at[0, pl.ds(at_col, ch), :], wg.at[k], w_sem.at[1, k]),
                    pltpu.make_async_copy(w_up.at[0, pl.ds(at_col, ch), :], wu.at[k], w_sem.at[2, k]),
                )
            )
        return downs, outs

    cot_copy = pltpu.make_async_copy(cot_hbm.at[0], cot, cot_sem.at[0])
    routes_copy = pltpu.make_async_copy(routes_hbm.at[0], routes, cot_sem.at[1])
    gates_copy = pltpu.make_async_copy(gates_hbm.at[0], gates, cot_sem.at[2])
    routes_copy.start()
    gates_copy.start()
    cot_copy.start()

    local_u = pltpu.make_async_copy(pre_u.at[0, :, 0], got_u.at[r], pre_rs.at[0, 0])
    local_v = pltpu.make_async_copy(pre_v.at[0, :, 0], got_v.at[r], pre_rs.at[1, 0])
    local_u.start()
    local_v.start()

    barrier = pltpu.get_barrier_semaphore()
    for o in range(1, n_src):
        q = lax.rem(me + o, n_src)
        pl.semaphore_signal(
            barrier, inc=1, device_id=at(p, lax.rem(q, n_dp), q // n_dp), device_id_type=MESH
        )

    @pl.when(p > 0)
    def _():
        for s in range(n_exp):
            pl.semaphore_signal(barrier, inc=1, device_id=at(p - 1, r, s), device_id_type=MESH)

    @pl.when(p < n_pipe - 1)
    def _():
        for s in range(n_exp):
            pl.semaphore_signal(barrier, inc=1, device_id=at(p + 1, r, s), device_id_type=MESH)

    routes_copy.wait()
    gates_copy.wait()
    local_u.wait()
    local_v.wait()

    @pl.when(p > 0)
    def _():
        downs, outs = weight_copies()
        for copy in downs:
            copy.start()
        for a, b in outs:
            a.start()
            b.start()

    sel0, g0 = slot_table(routes[0], gates[0].astype(F32), cap)
    sel1, g1 = slot_table(routes[1], gates[1].astype(F32), cap)
    sel_send[:, 0 : sel1.shape[1]] = sel1
    cot_copy.wait()

    for d in range(n_dp):
        rows = jnp.dot(
            sel0.astype(BF16), cot[:, d * half : (d + 1) * half], preferred_element_type=F32
        )
        for e in range(EXP_FL):
            send_rows[d, e, :, 0:half] = rows[e * cap : (e + 1) * cap].astype(BF16)
            send_rows[d, e, :, half : half + LANES] = g0[e * cap : (e + 1) * cap].astype(BF16)
            send_rows[d, e, :, half + LANES : half + 2 * LANES] = g1[e * cap : (e + 1) * cap].astype(BF16)
    recv_rows[me] = send_rows[r, j // split]

    above = (p + n_pipe - 1) // n_pipe
    below = (2 * n_pipe - 2 - p) // n_pipe
    pl.semaphore_wait(barrier, n_src - 1 + n_exp * (above + below))

    def rows_copy(o):
        q = lax.rem(me + o, n_src)
        dp_q, exp_q = lax.rem(q, n_dp), q // n_dp
        return remote(
            send_rows.at[dp_q, exp_q // split], recv_rows.at[me], rows_ss.at[o], rows_rs.at[me], at(p, dp_q, exp_q)
        )

    def rows_got(o):
        q = lax.rem(me + o, n_src)
        return remote(
            send_rows.at[0, 0], recv_rows.at[q], rows_ss.at[o], rows_rs.at[q], at(p, lax.rem(q, n_dp), q // n_dp)
        )

    for o in range(1, n_src):
        rows_copy(o).start()

    def sel_copy():
        return remote(sel_send, sel_recv, sel_ss.at[0], sel_rs.at[0], at(p + 1, r, j))

    @pl.when(p < n_pipe - 1)
    def _():
        sel_copy().start()

    def pre_copies(o):
        d = lax.rem(r + o, n_dp)
        return (
            remote(got_u.at[r], got_u.at[r], pre_ss.at[0, o], pre_rs.at[0, o], at(p, d, j)),
            remote(got_v.at[r], got_v.at[r], pre_ss.at[1, o], pre_rs.at[1, o], at(p, d, j)),
        )

    for o in range(1, n_dp):
        for copy in pre_copies(o):
            copy.start()

    def base_copy(o):
        d = lax.rem(r + o, n_dp)
        return remote(base_send.at[d], base_recv.at[r], base_ss.at[o], base_rs.at[o], at(p, d, j))

    @pl.when(p > 0)
    def _():
        sel_p = remote(sel_send, sel_recv, sel_ss.at[0], sel_rs.at[0], at(p - 1, r, j))
        sel_p.wait_recv()
        nxt = sel_recv[:, 0 : sel0.shape[1]]
        mapping = contract_last(nxt, sel0)
        pad = jnp.zeros((8, LANES - mapping.shape[1]), F32)
        mapping = jnp.concatenate([mapping, pad], axis=1)
        for d in range(n_dp):
            base_send[d, :, 0:half] = jnp.dot(
                nxt.astype(BF16), cot[:, d * half : (d + 1) * half], preferred_element_type=F32
            )
            base_send[d, :, half : half + LANES] = mapping
        base_recv[r] = base_send[r]
        for o in range(1, n_dp):
            base_copy(o).start()

    def acc_copy(h, o):
        d = lax.rem(r + o, n_dp)
        return remote(
            acc_send.at[h], acc_recv.at[h, o], acc_ss.at[h, o], acc_rs.at[h, o], at(p, d, j)
        )

    for o in range(1, n_src):
        rows_got(o).wait_recv()
    for q in range(n_src):
        stage_x[q * cap : (q + 1) * cap, :] = recv_rows[q].astype(F32)
    x = stage_x[:, 0:half].astype(BF16)
    out_rows[0:slots, :] = x

    @pl.when(p > 0)
    def _():
        downs, _ = weight_copies()
        for k in range(n_ch):
            downs[k].wait()
        for h in range(n_h):
            if fast:
                pieces = []
                for i in range(h * part_h, (h + 1) * part_h, step_h):
                    both = None
                    for k in range(n_ch):
                        term = rows_dot(
                            stage_x[:, k * ch : (k + 1) * ch].astype(BF16), wd.at[k], i, step_h, slice(0, ch)
                        )
                        both = term if both is None else both + term
                    pieces.append(rows_out(both, slots))
                acc_send[h] = jnp.concatenate(pieces, axis=1)
            else:
                acc = jnp.zeros((slots, part_h), F32)
                for k in range(n_ch):
                    acc = acc + contract_last(
                        stage_x[:, k * ch : (k + 1) * ch].astype(BF16), wd[k, h * part_h : (h + 1) * part_h, :]
                    )
                acc_send[h] = acc
            for o in range(1, n_dp):
                acc_copy(h, o).start()

    for o in range(1, n_dp):
        for copy in pre_copies(o):
            copy.wait_recv()
    for t in range(STEPS):
        for s in range(n_exp):
            for d in range(n_dp):
                row = t * slots + (s * n_dp + d) * cap
                stage_u[row : row + cap, :] = got_u[d, t, s].astype(F32)
                stage_v[row : row + cap, :] = got_v[d, t, s].astype(F32)
    for t in range(STEPS):
        u = stage_u[t * slots : (t + 1) * slots, :]
        v = stage_v[t * slots : (t + 1) * slots, :]
        g = stage_x[:, half + t * LANES : half + t * LANES + 1]
        out_scaled[t * slots : (t + 1) * slots, :] = (g * (u * jax.nn.sigmoid(u)) * v).astype(BF16)

    def part_copy(k, o):
        s = lax.rem(j + o, n_exp)
        return remote(
            part_send.at[k, s], part_recv.at[k, j], part_ss.at[k, o], part_rs.at[k, o], at(p, r, s)
        )

    def part_got(k, o):
        s = lax.rem(j + n_exp - o, n_exp)
        return remote(
            part_send.at[k, s], part_recv.at[k, s], part_ss.at[k, o], part_rs.at[k, o], at(p, r, s)
        )

    def fin_copy(k, s):
        return remote(
            fin_send.at[k, s // split], fin_recv.at[k, j], fin_ss.at[k, s], fin_rs.at[k, j], at(p - 1, r, s)
        )

    @pl.when(p > 0)
    def _():
        _, outs = weight_copies()

        def pre_grads(h):
            at_h = slice(h * part_h, (h + 1) * part_h)
            u = stage_u[0:slots, at_h]
            v = stage_v[0:slots, at_h]
            g = stage_x[:, half : half + 1]
            sig = jax.nn.sigmoid(u)
            total = acc_send[h]
            for o in range(1, n_dp):
                acc_copy(h, o).wait_recv()
                total = total + acc_recv[h, o]
            d_act = g * total
            d_gate = (d_act * v * (sig * (1.0 + u * (1.0 - sig)))).astype(BF16)
            d_up = (d_act * (u * sig)).astype(BF16)
            return d_gate, d_up

        def shares_of(k, d_gate, d_up):
            if not fast:
                yield contract_last(d_gate, wg[k]) + contract_last(d_up, wu[k])
                return
            everything = slice(0, hidden)
            for i in range(0, ch, step_c):
                yield rows_out(
                    rows_dot(d_gate, wg.at[k], i, step_c, everything)
                    + rows_dot(d_up, wu.at[k], i, step_c, everything),
                    slots,
                )

        def send_parts(k, pieces):
            part = jnp.concatenate(pieces, axis=1)
            for s in range(n_exp):
                part_send[k, s] = part[s * group : (s + 1) * group].astype(BF16)
            part_recv[k, j] = part_send[k, j]
            for o in range(1, n_exp):
                part_copy(k, o).start()

        for k in range(n_ch):
            outs[k][0].wait()
            outs[k][1].wait()
        d_gate, d_up = pre_grads(n_h - 1)
        ready = None
        for k in range(n_ch):
            pieces = []
            for i, piece in enumerate(shares_of(k, d_gate, d_up)):
                pieces.append(piece)
                if ready is not None and i == 1:
                    send_parts(*ready)
                    ready = None
            if ready is not None:
                send_parts(*ready)
            ready = (k, pieces)
        send_parts(*ready)
        for o in range(1, n_dp):
            base_copy(o).wait_recv()

        def reduce(k):
            for o in range(1, n_exp):
                part_got(k, o).wait_recv()
            sums = []
            for e in range(EXP_FL):
                value = part_recv[k, e * split].astype(F32)
                for i in range(1, split):
                    value = value + part_recv[k, e * split + i].astype(F32)
                sums.append(value)
            for d in range(n_dp):
                new = base_recv[d, :, k * ch : (k + 1) * ch]
                for e in range(EXP_FL):
                    for c in range(cap):
                        at_slot = half + e * cap + c
                        row = d * cap + c
                        new = new + base_recv[d, :, at_slot : at_slot + 1] * sums[e][row : row + 1]
                for e in range(EXP_FL):
                    fin_stage[e, d * cap : (d + 1) * cap, :] = new[e * cap : (e + 1) * cap]
            for e in range(EXP_FL):
                fin_send[k, e] = fin_stage[e].astype(BF16)
            for s in range(n_exp):
                fin_copy(k, s).start()

        for k in range(n_ch):
            reduce(k)

    @pl.when(p < n_pipe - 1)
    def _():
        for k in range(n_ch):
            for s in range(n_exp):
                remote(
                    fin_send.at[k, 0], fin_recv.at[k, s], fin_ss.at[k, s], fin_rs.at[k, s], at(p + 1, r, s)
                ).wait_recv()
            for s in range(n_exp):
                stage_x[s * group : (s + 1) * group, k * ch : (k + 1) * ch] = fin_recv[k, s].astype(F32)
        out_rows[slots : 2 * slots, :] = stage_x[:, 0:half].astype(BF16)

    @pl.when(p == n_pipe - 1)
    def _():
        out_rows[slots : 2 * slots, :] = jnp.zeros((slots, half), BF16)

    for o in range(1, n_src):
        rows_copy(o).wait_send()
    for o in range(1, n_dp):
        for copy in pre_copies(o):
            copy.wait_send()

    @pl.when(p < n_pipe - 1)
    def _():
        sel_copy().wait_send()

    @pl.when(p > 0)
    def _():
        for o in range(1, n_dp):
            base_copy(o).wait_send()
            for h in range(n_h):
                acc_copy(h, o).wait_send()
        for k in range(n_ch):
            for o in range(1, n_exp):
                part_copy(k, o).wait_send()
            for s in range(n_exp):
                fin_copy(k, s).wait_send()


def output_blocks(rows):
    sizes = [16, 16, 32, 64]
    sizes += [LANES] * (rows // LANES - 1)
    return [(sum(sizes[:i]), size) for i, size in enumerate(sizes)]


def output_kernel(rows, scaled, out, held, sem):
    right = rows[...]
    copies = []
    for i, (first, size) in enumerate(output_blocks(out.shape[1])):
        at = pl.ds(first, size)
        held[at, :] = lax.dot_general(
            scaled[:, at], right, (((0,), (0,)), ((), ())), preferred_element_type=F32
        )
        copies.append(pltpu.make_async_copy(held.at[at, :], out.at[0, at, :], sem.at[i]))
        copies[-1].start()
    for copy in copies:
        copy.wait()


def body(mesh_shape, cotangent, routes, gates, gate_pre, up_pre, w_gate, w_up, w_down):
    n_pipe, n_dp, n_exp = mesh_shape
    width = cotangent.shape[2]
    cap = gate_pre.shape[4]
    hidden = gate_pre.shape[5]
    half = width // n_dp
    n_ch = 2
    ch = half // n_ch
    n_h = 1
    n_src = n_dp * n_exp
    slots = n_src * cap
    group = n_dp * cap
    dims = (n_pipe, n_dp, n_exp, cap, width, hidden, n_ch)
    vmem = pl.BlockSpec(memory_space=pltpu.VMEM)
    hbm = pl.BlockSpec(memory_space=pltpu.HBM)
    dma = pltpu.SemaphoreType.DMA
    rows, scaled = pl.pallas_call(
        functools.partial(kernel, dims),
        out_shape=(
            pltpu.VMEM((STEPS * slots, half), BF16),
            pltpu.VMEM((STEPS * slots, hidden), BF16),
        ),
        in_specs=[hbm, hbm, hbm, hbm, hbm, hbm, hbm, hbm],
        out_specs=(vmem, vmem),
        scratch_shapes=[
            pltpu.VMEM((cotangent.shape[1], width), BF16),
            pltpu.VMEM((STEPS, routes.shape[3], routes.shape[2]), jnp.int32),
            pltpu.VMEM((STEPS, routes.shape[3], routes.shape[2]), BF16),
            pltpu.VMEM((n_ch, hidden, ch), BF16),
            pltpu.VMEM((n_ch, ch, hidden), BF16),
            pltpu.VMEM((n_ch, ch, hidden), BF16),
            pltpu.VMEM((n_dp, STEPS, n_exp, cap, hidden), BF16),
            pltpu.VMEM((n_dp, STEPS, n_exp, cap, hidden), BF16),
            pltpu.VMEM((STEPS * slots, hidden), F32),
            pltpu.VMEM((STEPS * slots, hidden), F32),
            pltpu.VMEM((n_dp, EXP_FL, cap, half + 2 * LANES), BF16),
            pltpu.VMEM((n_src, cap, half + 2 * LANES), BF16),
            pltpu.VMEM((slots, half + 2 * LANES), F32),
            pltpu.VMEM((8, LANES), F32),
            pltpu.VMEM((8, LANES), F32),
            pltpu.VMEM((n_dp, 8, half + LANES), F32),
            pltpu.VMEM((n_dp, 8, half + LANES), F32),
            pltpu.VMEM((n_h, slots, hidden // n_h), F32),
            pltpu.VMEM((n_h, n_dp, slots, hidden // n_h), F32),
            pltpu.VMEM((n_ch, n_exp, group, ch), BF16),
            pltpu.VMEM((n_ch, n_exp, group, ch), BF16),
            pltpu.VMEM((EXP_FL, group, ch), F32),
            pltpu.VMEM((n_ch, EXP_FL, group, ch), BF16),
            pltpu.VMEM((n_ch, n_exp, group, ch), BF16),
            dma((3,)),
            dma((3, n_ch)),
            dma((2, n_dp)),
            dma((2, n_dp)),
            dma((n_src,)),
            dma((n_src,)),
            dma((1,)),
            dma((1,)),
            dma((n_dp,)),
            dma((n_dp,)),
            dma((n_h, n_dp)),
            dma((n_h, n_dp)),
            dma((n_ch, n_exp)),
            dma((n_ch, n_exp)),
            dma((n_ch, n_exp)),
            dma((n_ch, n_exp)),
        ],
        compiler_params=pltpu.CompilerParams(
            collective_id=0, has_side_effects=True, vmem_limit_bytes=58 * 1024 * 1024
        ),
    )(cotangent, jnp.swapaxes(routes, 2, 3), jnp.swapaxes(gates, 2, 3), gate_pre, up_pre, w_gate, w_up, w_down)
    total = pl.pallas_call(
        output_kernel,
        out_shape=jax.ShapeDtypeStruct((1, hidden, half), F32),
        in_specs=[vmem, vmem],
        out_specs=hbm,
        scratch_shapes=[pltpu.VMEM((hidden, half), F32), dma((len(output_blocks(hidden)),))],
        compiler_params=pltpu.CompilerParams(vmem_limit_bytes=60 * 1024 * 1024),
    )(pltpu.with_memory_space_constraint(rows, pltpu.VMEM), pltpu.with_memory_space_constraint(scaled, pltpu.VMEM))
    return total


def solution(mesh):
    mesh_shape = (mesh.shape["pipe"], mesh.shape["dp"], mesh.shape["expert"])
    in_specs = (
        P("pipe", ("dp", "expert"), None),
        P("pipe", None, ("dp", "expert"), None),
        P("pipe", None, ("dp", "expert"), None),
        P("pipe", None, "dp", None, None, "expert"),
        P("pipe", None, "dp", None, None, "expert"),
        P("pipe", None, "expert"),
        P("pipe", None, "expert"),
        P("pipe", "expert", None),
    )
    out_specs = P("pipe", "expert", "dp")
    return jax.shard_map(
        functools.partial(body, mesh_shape), mesh=mesh, in_specs=in_specs, out_specs=out_specs, check_vma=False
    )
```

profile of v0, /device:TPU:0, one launch (start us, length us, event | category | flops | bytes accessed | tf_op | source)
XLA Modules:
  0.0 26.8 jit_solution(10565173373571077215)
XLA Ops:
  0.0 21.3 %shard_map.82 = (bf16[32,3584]{1,0:T(8,128)(2,1)S(1)}, bf16[32,1024]{1,0:T(8,128)(2,1)S(1)}) custom-call(bf16[1,64,7168]{2,1,0:T(8,128)(2,1)} %cot_hbm.1, s32[1,2,8,64]{3,2,1,0:T(8,128)} %bitcast.2, bf16[1,2,8,64]{3,2,1,0:T(8,128)(2,1)} %bitcast.3, bf16[1,2,1,4,2,1024]{5,4,3,2,1,0:T(2,128)(2,1)} %pre_u.1, bf16[1,2,1,4,2,1024]{5,4,3,2,1,0:T(2,128)(2,1)} %pre_v.1, ...), custom_call_target="tpu_custom_call" | custom-call | tf_op jit(solution)/shard_map/pallas_call | solution.py:505
  21.3 5.6 %shard_map.83 = f32[1,1024,3584]{2,1,0:T(8,128)} custom-call(bf16[32,3584]{1,0:T(8,128)(2,1)S(1)} %get-tuple-element.7.rows, bf16[32,1024]{1,0:T(8,128)(2,1)S(1)} %get-tuple-element.8.scaled), custom_call_target="tpu_custom_call" | custom-call | tf_op jit(solution)/shard_map/pallas_call | solution.py:559
where the time goes:
time: 27 us; the launch traced here: 26.8 us
  Pallas kernels  26.8 us (99%)
    pallas_call x1, Pallas kernels, body(): pl.pallas_call(functools.partial(kernel, dims), out_shape=(pltpu.VMEM((ST...  21.3 us
    pallas_call x1, Pallas kernels, body(): pl.pallas_call(output_kernel, out_shape=jax.ShapeDtypeStruct((1, hidden,...  5.57 us

commit v1 on v0

--- a/solution.py
+++ b/solution.py
@@ -10,6 +10,7 @@
 EXP_FL = 2
 STEPS = 2
 LANES = 128
+STEP = 512
 MESH = pl.DeviceIdType.MESH
 F32 = jnp.float32
 BF16 = jnp.bfloat16
@@ -23,7 +24,7 @@
 
 def steps_of(size):
     for count in range(2, size // 32 + 1, 2):
-        if size % count == 0 and size // count % 16 == 0 and size // count <= 448:
+        if size % count == 0 and size // count % 16 == 0 and size // count <= STEP:
             return size // count
     return 0
 
@@ -129,6 +130,9 @@
     fast = slots == 16 and step_h > 64 and step_c > 64 and part_h % LANES == 0
     p, r, j = lax.axis_index("pipe"), lax.axis_index("dp"), lax.axis_index("expert")
     me = j * n_dp + r
+    far = lax.rem(2 * n_exp - 1 - 2 * j, n_exp)
+    offsets = [lax.rem(far + i, n_exp) for i in range(0, n_exp, 2)] + list(range(2, n_exp, 2))
+    peers = [(o, d) for o in offsets for d in range(n_dp)] + [(0, d) for d in range(1, n_dp)]
 
     def at(pipe, dp, expert):
         return {"pipe": pipe, "dp": dp, "expert": expert}
@@ -167,6 +171,15 @@
     local_u.start()
     local_v.start()
 
+    @pl.when(p > 0)
+    def _():
+        downs, outs = weight_copies()
+        for copy in downs:
+            copy.start(priority=1)
+        for a, b in outs:
+            a.start(priority=1)
+            b.start(priority=1)
+
     barrier = pltpu.get_barrier_semaphore()
     for o in range(1, n_src):
         q = lax.rem(me + o, n_src)
@@ -176,28 +189,14 @@
 
     @pl.when(p > 0)
     def _():
-        for s in range(n_exp):
-            pl.semaphore_signal(barrier, inc=1, device_id=at(p - 1, r, s), device_id_type=MESH)
+        pl.semaphore_signal(barrier, inc=1, device_id=at(p - 1, r, j), device_id_type=MESH)
 
     @pl.when(p < n_pipe - 1)
     def _():
-        for s in range(n_exp):
-            pl.semaphore_signal(barrier, inc=1, device_id=at(p + 1, r, s), device_id_type=MESH)
+        pl.semaphore_signal(barrier, inc=1, device_id=at(p + 1, r, j), device_id_type=MESH)
 
     routes_copy.wait()
     gates_copy.wait()
-    local_u.wait()
-    local_v.wait()
-
-    @pl.when(p > 0)
-    def _():
-        downs, outs = weight_copies()
-        for copy in downs:
-            copy.start()
-        for a, b in outs:
-            a.start()
-            b.start()
-
     sel0, g0 = slot_table(routes[0], gates[0].astype(F32), cap)
     sel1, g1 = slot_table(routes[1], gates[1].astype(F32), cap)
     sel_send[:, 0 : sel1.shape[1]] = sel1
@@ -215,23 +214,25 @@
 
     above = (p + n_pipe - 1) // n_pipe
     below = (2 * n_pipe - 2 - p) // n_pipe
-    pl.semaphore_wait(barrier, n_src - 1 + n_exp * (above + below))
-
-    def rows_copy(o):
-        q = lax.rem(me + o, n_src)
-        dp_q, exp_q = lax.rem(q, n_dp), q // n_dp
+    pl.semaphore_wait(barrier, n_src - 1 + above + below)
+
+    def peer(i):
+        o, d = peers[i]
+        return lax.rem(r + d, n_dp), lax.rem(j + o, n_exp)
+
+    def rows_copy(i):
+        dp_q, exp_q = peer(i)
         return remote(
-            send_rows.at[dp_q, exp_q // split], recv_rows.at[me], rows_ss.at[o], rows_rs.at[me], at(p, dp_q, exp_q)
-        )
-
-    def rows_got(o):
-        q = lax.rem(me + o, n_src)
-        return remote(
-            send_rows.at[0, 0], recv_rows.at[q], rows_ss.at[o], rows_rs.at[q], at(p, lax.rem(q, n_dp), q // n_dp)
-        )
-
-    for o in range(1, n_src):
-        rows_copy(o).start()
+            send_rows.at[dp_q, exp_q // split], recv_rows.at[me], rows_ss.at[i], rows_rs.at[me], at(p, dp_q, exp_q)
+        )
+
+    def rows_got(i):
+        dp_q, exp_q = peer(i)
+        q = exp_q * n_dp + dp_q
+        return remote(send_rows.at[0, 0], recv_rows.at[q], rows_ss.at[i], rows_rs.at[q], at(p, dp_q, exp_q))
+
+    for i in range(n_src - 1):
+        rows_copy(i).start()
 
     def sel_copy():
         return remote(sel_send, sel_recv, sel_ss.at[0], sel_rs.at[0], at(p + 1, r, j))
@@ -247,6 +248,8 @@
             remote(got_v.at[r], got_v.at[r], pre_ss.at[1, o], pre_rs.at[1, o], at(p, d, j)),
         )
 
+    local_u.wait()
+    local_v.wait()
     for o in range(1, n_dp):
         for copy in pre_copies(o):
             copy.start()
@@ -278,8 +281,8 @@
             acc_send.at[h], acc_recv.at[h, o], acc_ss.at[h, o], acc_rs.at[h, o], at(p, d, j)
         )
 
-    for o in range(1, n_src):
-        rows_got(o).wait_recv()
+    for i in range(n_src - 1):
+        rows_got(i).wait_recv()
     for q in range(n_src):
         stage_x[q * cap : (q + 1) * cap, :] = recv_rows[q].astype(F32)
     x = stage_x[:, 0:half].astype(BF16)
@@ -380,7 +383,7 @@
             for s in range(n_exp):
                 part_send[k, s] = part[s * group : (s + 1) * group].astype(BF16)
             part_recv[k, j] = part_send[k, j]
-            for o in range(1, n_exp):
+            for o in offsets:
                 part_copy(k, o).start()
 
         for k in range(n_ch):
@@ -422,8 +425,8 @@
                     fin_stage[e, d * cap : (d + 1) * cap, :] = new[e * cap : (e + 1) * cap]
             for e in range(EXP_FL):
                 fin_send[k, e] = fin_stage[e].astype(BF16)
-            for s in range(n_exp):
-                fin_copy(k, s).start()
+            for o in offsets + [0]:
+                fin_copy(k, lax.rem(j + o, n_exp)).start()
 
         for k in range(n_ch):
             reduce(k)
@@ -443,8 +446,8 @@
     def _():
         out_rows[slots : 2 * slots, :] = jnp.zeros((slots, half), BF16)
 
-    for o in range(1, n_src):
-        rows_copy(o).wait_send()
+    for i in range(n_src - 1):
+        rows_copy(i).wait_send()
     for o in range(1, n_dp):
         for copy in pre_copies(o):
             copy.wait_send()

time: 27 us -> 26.6 us (0.985)
  Pallas kernels: 26.8 us -> 26.4 us
    pallas_call x1, Pallas kernels: 21.3 us -> 20.8 us  [body(): pl.pallas_call(functools.partial(kernel, dims), out_shape=(pltpu.VMEM((ST...]
where the time goes in v1:
time: 26.6 us; the launch traced here: 26.4 us
  Pallas kernels  26.4 us (99%)
    pallas_call x1, Pallas kernels, body(): pl.pallas_call(functools.partial(kernel, dims), out_shape=(pltpu.VMEM((ST...  20.8 us
    pallas_call x1, Pallas kernels, body(): pl.pallas_call(output_kernel, out_shape=jax.ShapeDtypeStruct((1, hidden,...  5.58 us

profile of v1, /device:TPU:0, one launch (start us, length us, event | category | flops | bytes accessed | tf_op | source)
XLA Modules:
  0.0 26.4 jit_solution(16730177081808174186)
XLA Ops:
  0.0 20.8 %shard_map.82 = (bf16[32,3584]{1,0:T(8,128)(2,1)S(1)}, bf16[32,1024]{1,0:T(8,128)(2,1)S(1)}) custom-call(bf16[1,64,7168]{2,1,0:T(8,128)(2,1)} %cot_hbm.1, s32[1,2,8,64]{3,2,1,0:T(8,128)} %bitcast.2, bf16[1,2,8,64]{3,2,1,0:T(8,128)(2,1)} %bitcast.3, bf16[1,2,1,4,2,1024]{5,4,3,2,1,0:T(2,128)(2,1)} %pre_u.1, bf16[1,2,1,4,2,1024]{5,4,3,2,1,0:T(2,128)(2,1)} %pre_v.1, ...), custom_call_target="tpu_custom_call" | custom-call | tf_op jit(solution)/shard_map/pallas_call | solution.py:508
  20.8 5.6 %shard_map.83 = f32[1,1024,3584]{2,1,0:T(8,128)} custom-call(bf16[32,3584]{1,0:T(8,128)(2,1)S(1)} %get-tuple-element.7.rows, bf16[32,1024]{1,0:T(8,128)(2,1)S(1)} %get-tuple-element.8.scaled), custom_call_target="tpu_custom_call" | custom-call | tf_op jit(solution)/shard_map/pallas_call | solution.py:562
